TPU v7x, 256 devices: a whole 4x4x8 slice. The times are simulated.
256 devices in a mesh: outer: 4 (over x), inner: 64 (over z, y, core).
Axes of the slice: x: 4, y: 4, z: 8, core: 2. Of those that a mesh axis runs over, the one named last changes fastest.
Arguments:
- prim: float32 [8, 3072, 512], P(None, ('outer', 'inner')), may hold values from -4 to 9, as said below
- new_owner: int32 [3072], replicated, may hold values from 0 to 255, as said below
- new_slot: int32 [3072], replicated, may hold values from 0 to 23, as said below
Outputs:
- placed: float32 [8, 6144, 512], P(None, ('outer', 'inner'))
Inputs may be any that keep to these rules, and one draw needn't show every extreme that they name: `prim`: field 0 (density) lies in 0.3 to 3 and field 4 (pressure) in 0.2 to 9; fields 1 to 3 are velocities and 5 to 7 the magnetic field. `new_owner`: block g's owner lies in the segment of 64 devices that holds device g // 12 and differs from g // 12 by at most one; owners never fall along g, so every device gets a run of consecutive blocks (possibly none); at most 6 blocks of one device go to each neighbour, and in every draw some device of each segment receives 24 blocks. `new_slot`: the blocks of one owner have slots 0, 1, 2, ... in the order of g.
All inputs are finite; a program needn't handle non-finite values.
Results may differ from a plain program's by a relative error of at most 0.0003.
Values sent between devices are 32-bit elements; how exact they have to be, the bound alone decides.
No kernel may reach another device: no remote copies, remote signals or barrier semaphores. Data moves between devices by JAX's collectives and lax.ppermute only.
A program may use at most 64 MiB of HBM per device.

v0:
```python
import functools

import jax
import jax.numpy as jnp
from jax import lax
from jax.experimental import pallas as pl
from jax.experimental.pallas import tpu as pltpu
from jax.sharding import PartitionSpec as P


BE = 8
GY = 16
AXES = ("outer", "inner")
GAMMA = 5.0 / 3.0
COURANT = 0.8
LANES = 128
TILES = 4
FIELDS = 8
BLOCKS = 12
REACH = 6
CAP = 24
ROWS = 16
HELD = 40
SIDE = FIELDS * 2 * BE
PITCH = BE + 2
APART = FIELDS + 1
CHUNKS = 4


def roll(value, shift):
    return pltpu.roll(value, shift % LANES, 1)


def half_minmod(former, latter):
    return 0.5 * (
        jnp.maximum(jnp.minimum(former, latter), 0.0)
        + jnp.minimum(jnp.maximum(former, latter), 0.0)
    )


def sound(density, pressure, field_sq):
    pushed = GAMMA * pressure + field_sq
    return pushed * lax.rsqrt(pushed * density)


def squared(state):
    return state[5] * state[5] + state[6] * state[6] + state[7] * state[7]


def conserved(state, field_sq):
    density, pressure = state[0], state[4]
    momentum = [density * state[1 + k] for k in range(3)]
    kinetic = momentum[0] * state[1] + momentum[1] * state[2] + momentum[2] * state[3]
    energy = pressure * (1.0 / (GAMMA - 1.0)) + 0.5 * (kinetic + field_sq)
    return [density, *momentum, energy, state[5], state[6], state[7]]


def flux_parts(state, normal):
    field_sq = squared(state)
    total_pressure = state[4] + 0.5 * field_sq
    whole = conserved(state, field_sq)
    speed, field = state[1 + normal], state[5 + normal]
    along = state[1] * state[5] + state[2] * state[6] + state[3] * state[7]
    momentum = [whole[1 + k] * speed - state[5 + k] * field for k in range(3)]
    momentum[normal] = momentum[normal] + total_pressure
    induction = [
        None if k == normal else state[5 + k] * speed - state[1 + k] * field for k in range(3)
    ]
    energy = (whole[4] + total_pressure) * speed - field * along
    signal = jnp.abs(speed) + sound(state[0], state[4], field_sq)
    return [whole[1 + normal], *momentum, energy, *induction], signal, whole


def twice_face_flux(left, right, normal):
    flux_left, signal_left, whole_left = flux_parts(left, normal)
    flux_right, signal_right, whole_right = flux_parts(right, normal)
    fastest = jnp.maximum(signal_left, signal_right)
    result = []
    for k in range(FIELDS):
        spread = fastest * (whole_right[k] - whole_left[k])
        result.append(-spread if flux_left[k] is None else flux_left[k] + flux_right[k] - spread)
    return result


def rows_of(index):
    return slice(index * ROWS, (index + 1) * ROWS)


def device_index():
    return lax.axis_index(AXES[0]) * lax.axis_size(AXES[1]) + lax.axis_index(AXES[1])


def turn(first, second):
    row = lax.broadcasted_iota(jnp.int32, (8, LANES), 0)
    group = lax.broadcasted_iota(jnp.int32, (8, LANES), 1) // 8

    def skewed(value, shift):
        return pltpu.roll(value, shift, 1, stride=8, stride_axis=0)

    def across(value, source):
        return jnp.take_along_axis(value, source, axis=0, mode="promise_in_bounds")

    first, second = skewed(first, 0), skewed(second, 64)

    def picked(index):
        source = (row + group + index) & 15
        return jnp.where(source < 8, across(first, source & 7), across(second, source & 7))

    upper, lower = skewed(picked(1), 8), skewed(picked(9), 72)
    return across(lower, 7 - row), across(upper, 7 - row)


def prepare_kernel(
    prim_ref,
    x_first_ref,
    x_second_ref,
    y_inner_ref,
    y_outer_ref,
    fastest_ref,
    cells_ref,
    whole_ref,
    raw_ref,
    spread_ref,
    filled_ref,
    arrived,
    left,
):
    device = device_index()
    odd_row = (device // GY) % 2 == 1
    odd = device % 2 == 1
    part = TILES * FIELDS * BLOCKS // CHUNKS
    copies = [
        pltpu.make_async_copy(
            prim_ref.at[pl.ds(i * part, part)], raw_ref.at[pl.ds(i * part, part)], arrived.at[i]
        )
        for i in range(CHUNKS)
    ]
    for copy in copies:
        copy.start()
    for block in range(BLOCKS):
        if block % (BLOCKS // CHUNKS) == 0:
            copies[block // (BLOCKS // CHUNKS)].wait()
        rows = [block]
        if block == 0:
            rows += [12, 13, 14]
        if block == BLOCKS - 1:
            rows += [15]
        for tile in range(TILES):
            value = raw_ref[(block * TILES + tile) * FIELDS : (block * TILES + tile + 1) * FIELDS]
            for row in rows:
                base = (tile * ROWS + row) * APART
                spread_ref[base : base + FIELDS] = value

    def cell(k, tile, half):
        return spread_ref[pl.ds((tile * ROWS + 8 * half) * APART + k, 8, stride=APART)]

    best = None
    for tile in range(TILES):
        for half in range(2):
            state = [cell(k, tile, half) for k in range(FIELDS)]
            field_sq = squared(state)
            speed = (
                jnp.abs(state[1])
                + jnp.abs(state[2])
                + jnp.abs(state[3])
                + 3.0 * sound(state[0], state[4], field_sq)
            )
            best = speed if best is None else jnp.maximum(best, speed)
            for k, value in enumerate(conserved(state, field_sq)):
                base = (k * TILES + tile) * ROWS + 8 * half
                whole_ref[base : base + 8] = value
    filled_ref[...] = jnp.broadcast_to(jnp.max(best, keepdims=True), filled_ref.shape)
    leaving = pltpu.make_async_copy(filled_ref, fastest_ref, left)
    leaving.start()
    for k in range(FIELDS):
        for tile in range(TILES):
            halves = turn(cell(k, tile, 0), cell(k, tile, 1))
            base = (k * BE + 2 * tile) * BE
            cells_ref[base : base + 8], cells_ref[base + 8 : base + 16] = halves
    to_first = jnp.where(odd_row, 0, BE - 2)
    to_second = jnp.where(odd_row, BE - 2, 0)
    to_inner = jnp.where(odd, 0, BE - 2)
    to_outer = jnp.where(odd, BE - 2, 0)
    for k in range(FIELDS):
        base, there = k * BE * BE, slice(k * 2 * BE, (k + 1) * 2 * BE)
        for start, ref in ((to_first, x_first_ref), (to_second, x_second_ref)):
            ref[there] = cells_ref[pl.ds(pl.multiple_of(base + start * BE, BE), 2 * BE)]
        for start, ref in ((to_inner, y_inner_ref), (to_outer, y_outer_ref)):
            for layer in range(2):
                row = (2 * k + layer) * BE
                ref[row : row + BE] = cells_ref[pl.ds(base + start + layer, BE, stride=BE)]
    send_half(whole_ref, y_inner_ref, y_outer_ref, SIDE, odd)
    leaving.wait()


def send_half(source, inner_ref, outer_ref, base, odd):
    to_inner = jnp.where(odd, 0, REACH)
    to_outer = jnp.where(odd, REACH, 0)
    for row in range(FIELDS * TILES):
        there = slice(base + row * REACH, base + (row + 1) * REACH)
        inner_ref[there] = source[pl.ds(row * ROWS + to_inner, REACH)]
        outer_ref[there] = source[pl.ds(row * ROWS + to_outer, REACH)]


def change_kernel(
    cells_ref,
    x_first_ref,
    x_second_ref,
    y_inner_ref,
    y_outer_ref,
    own_ref,
    inner_ref,
    outer_ref,
    line_ref,
    right_ref,
    face_ref,
):
    device = device_index()
    odd_row = (device // GY) % 2 == 1
    odd = device % 2 == 1
    fields = range(FIELDS)

    def cell(x, k):
        return cells_ref[(k * BE + x) * BE : (k * BE + x + 1) * BE]

    def halo(first, second, k, layer, flag):
        rows = slice((2 * k + layer) * BE, (2 * k + layer + 1) * BE)
        return jnp.where(flag, first[rows], second[rows])

    def padded(x, k, y):
        return slice((k * BE + x) * PITCH + y + 1, (k * BE + x) * PITCH + y + 1 + BE)

    def all_x(k, y):
        return pl.ds(k * BE * PITCH + y + 1, BE, stride=PITCH)

    def column(x):
        if x < 0:
            return [halo(x_first_ref, x_second_ref, k, x + 2, odd_row) for k in fields]
        if x >= BE:
            return [halo(x_second_ref, x_first_ref, k, x - BE, odd_row) for k in fields]
        return [cell(x, k) for k in fields]

    total = [None] * BE
    here, up = column(-2), column(-1)
    ahead = [up[k] - here[k] for k in fields]
    left = last_face = None
    for x in range(-1, BE + 1):
        here, up, behind = up, column(x + 1), ahead
        ahead = [up[k] - here[k] for k in fields]
        half = [half_minmod(behind[k], ahead[k]) for k in fields]
        if left is not None:
            face = twice_face_flux(left, [here[k] - half[k] for k in fields], 0)
            if last_face is not None:
                total[x - 1] = [face[k] - last_face[k] for k in fields]
            last_face = face
        left = [here[k] + half[k] for k in fields]

    low_left, low_right = [], []
    for k in fields:
        far = halo(y_inner_ref, y_outer_ref, k, 0, odd)
        near = halo(y_inner_ref, y_outer_ref, k, 1, odd)
        edge = cells_ref[pl.ds(k * BE * BE, BE, stride=BE)]
        after = cells_ref[pl.ds(k * BE * BE + 1, BE, stride=BE)]
        low_left.append(near + half_minmod(near - far, edge - near))
        low_right.append(edge - half_minmod(edge - near, after - edge))
        line_ref[all_x(k, -1)] = near
        near = halo(y_outer_ref, y_inner_ref, k, 0, odd)
        far = halo(y_outer_ref, y_inner_ref, k, 1, odd)
        edge = cells_ref[pl.ds(k * BE * BE + BE - 1, BE, stride=BE)]
        line_ref[all_x(k, BE)] = near
        right_ref[all_x(k, BE)] = near - half_minmod(near - edge, far - near)
    for k, value in enumerate(twice_face_flux(low_left, low_right, 1)):
        face_ref[all_x(k, -1)] = value
    for x in range(BE):
        for k in fields:
            line_ref[padded(x, k, 0)] = cell(x, k)
    for x in range(BE):
        state = [cell(x, k) for k in fields]
        left = []
        for k in fields:
            half = half_minmod(
                state[k] - line_ref[padded(x, k, -1)], line_ref[padded(x, k, 1)] - state[k]
            )
            left.append(state[k] + half)
            right_ref[padded(x, k, 0)] = state[k] - half
        face = twice_face_flux(left, [right_ref[padded(x, k, 1)] for k in fields], 1)
        for k in fields:
            face_ref[padded(x, k, 0)] = face[k]
        for k in fields:
            total[x][k] = total[x][k] + (face[k] - face_ref[padded(x, k, -1)])

        left, right = [], []
        for k in fields:
            ahead = roll(state[k], -1) - state[k]
            half = half_minmod(roll(ahead, 1), ahead)
            left.append(state[k] + half)
            right.append(roll(state[k] - half, -1))
        face = twice_face_flux(left, right, 2)
        for k in fields:
            total[x][k] = total[x][k] + (face[k] - roll(face[k], 1))

    for k in fields:
        for tile in range(TILES):
            base = (k * TILES + tile) * ROWS
            halves = turn(total[2 * tile][k], total[2 * tile + 1][k])
            own_ref[base : base + 8], own_ref[base + 8 : base + 16] = halves
    send_half(own_ref, inner_ref, outer_ref, 0, odd)


def place_kernel(
    fastest_ref,
    whole_ref,
    change_ref,
    whole_inner_ref,
    whole_outer_ref,
    inner_ref,
    outer_ref,
    owner_ref,
    out_ref,
    held_ref,
    ready_ref,
    left,
):
    device = device_index()
    odd = device % 2 == 1
    owners = owner_ref[...]
    first = jnp.sum((owners < device).astype(jnp.int32)) - (device * BLOCKS - REACH)
    count = jnp.sum((owners == device).astype(jnp.int32))
    first = jnp.clip(first, 0, BLOCKS) + 2
    scale = (0.5 * COURANT) / jnp.max(fastest_ref[...])
    live = lax.broadcasted_iota(jnp.int32, (CAP, LANES), 0) < count
    for row in range(FIELDS * TILES):
        there = slice(row * REACH, (row + 1) * REACH)
        sent = slice(SIDE + row * REACH, SIDE + (row + 1) * REACH)
        inner = whole_inner_ref[sent] - scale * inner_ref[there]
        outer = whole_outer_ref[sent] - scale * outer_ref[there]
        base = row * HELD
        held_ref[base + 8 : base + 8 + ROWS] = (
            whole_ref[rows_of(row)] - scale * change_ref[rows_of(row)]
        )
        held_ref[base + 2 : base + 8] = jnp.where(odd, inner, outer)
        held_ref[base + 20 : base + 26] = jnp.where(odd, outer, inner)
    copies = []
    for row in range(FIELDS * TILES):
        k, tile = divmod(row, TILES)
        value = held_ref[pl.ds(row * HELD + first, CAP)]
        ready_ref[k, :, tile * LANES : (tile + 1) * LANES] = jnp.where(live, value, 0.0)
        if (row + 1) % (2 * TILES) == 0:
            two = pl.ds(k - 1, 2)
            copies.append(
                pltpu.make_async_copy(ready_ref.at[two], out_ref.at[two], left.at[k // 2])
            )
            copies[-1].start()
    for copy in copies:
        copy.wait()


HBM = pl.BlockSpec(memory_space=pltpu.HBM)
VMEM = pl.BlockSpec(memory_space=pltpu.VMEM)


def call(kernel, ins, outs, flops, scratch=()):
    return pl.pallas_call(
        kernel,
        out_shape=[
            jax.ShapeDtypeStruct(out if isinstance(out, tuple) else (out, LANES), jnp.float32)
            for out, _ in outs
        ],
        in_specs=list(ins),
        out_specs=[place for _, place in outs],
        scratch_shapes=list(scratch),
        cost_estimate=pl.CostEstimate(flops=flops, bytes_accessed=flops // 8, transcendentals=0),
        compiler_params=pltpu.CompilerParams(vmem_limit_bytes=8 * 2**20),
    )


def room(rows):
    return pltpu.VMEM((rows, LANES), jnp.float32)


def swap(value, partner, devices):
    pairs = [(i, partner(i) % devices) for i in range(devices) if partner(i) is not None]
    return lax.ppermute(value, AXES, pairs)


def per_device(ranks, prim, new_owner, new_slot):
    del new_slot
    devices = lax.axis_size(AXES)
    raw = prim.reshape(FIELDS, BLOCKS, TILES, LANES).transpose(1, 2, 0, 3).reshape(-1, LANES)
    half = FIELDS * TILES * REACH
    whole = FIELDS * TILES * ROWS
    x_first, x_second, y_inner, y_outer, fastest, cells, conserved_own = call(
        prepare_kernel,
        [HBM],
        [
            (SIDE, VMEM),
            (SIDE, VMEM),
            (SIDE + half, VMEM),
            (SIDE + half, VMEM),
            (devices, HBM),
            (FIELDS * BE * BE, VMEM),
            (whole, VMEM),
        ],
        10**6,
        [
            room(FIELDS * TILES * BLOCKS),
            room(TILES * ROWS * APART),
            room(devices),
            pltpu.SemaphoreType.DMA((CHUNKS,)),
            pltpu.SemaphoreType.DMA,
        ],
    )(pltpu.with_memory_space_constraint(raw, pltpu.HBM))
    everyone = lax.all_to_all(fastest, AXES, 0, 0, tiled=True)

    def within(i, j):
        return j if 0 <= j < devices and i // ranks == j // ranks else None

    x_first = swap(x_first, lambda i: i + GY if (i // GY) % 2 == 0 else i - GY, devices)
    x_second = swap(x_second, lambda i: i + GY if (i // GY) % 2 == 1 else i - GY, devices)
    y_outer = swap(y_outer, lambda i: i + 1 if i % 2 == 1 else i - 1, devices)
    y_inner = swap(y_inner, lambda i: i ^ 1, devices)
    own, to_inner, to_outer = call(
        change_kernel,
        [VMEM] * 5,
        [(whole, VMEM), (half, VMEM), (half, VMEM)],
        2 * 10**7,
        [room(FIELDS * BE * PITCH)] * 3,
    )(cells, x_first, x_second, y_inner, y_outer)
    from_outer = swap(to_outer, lambda i: within(i, i + 1 if i % 2 == 1 else i - 1), devices)
    from_inner = swap(to_inner, lambda i: i ^ 1, devices)
    (placed,) = call(
        place_kernel,
        [VMEM] * 8,
        [((FIELDS, CAP, TILES * LANES), HBM)],
        10**6,
        [
            room(FIELDS * TILES * HELD),
            pltpu.VMEM((FIELDS, CAP, TILES * LANES), jnp.float32),
            pltpu.SemaphoreType.DMA((FIELDS // 2,)),
        ],
    )(
        everyone,
        conserved_own,
        own,
        y_inner,
        y_outer,
        from_inner,
        from_outer,
        new_owner.reshape(-1, LANES),
    )
    return placed


def solution(mesh):
    return jax.shard_map(
        functools.partial(per_device, mesh.shape["inner"]),
        mesh=mesh,
        in_specs=(P(None, AXES, None), P(), P()),
        out_specs=P(None, AXES, None),
        check_vma=False,
    )
```

profile of v0, /device:TPU:57, one launch (start us, length us, event | category | flops | bytes accessed | tf_op | source)
XLA Modules:
  0.0 41.8 jit_solution(13743803357771696163)
XLA Ops:
  0.0 1.8 %shard_map.28 = (f32[128,128]{1,0:T(8,128)S(1)}, f32[128,128]{1,0:T(8,128)S(1)}, f32[320,128]{1,0:T(8,128)S(1)}, f32[320,128]{1,0:T(8,128)S(1)}, f32[256,128]{1,...) custom-call(f32[384,128]{1,0:T(8,128)} %bitcast.12), custom_call_target="tpu_custom_call" | custom-call | flops 1000000 | bytes 125000 | tf_op jit(solution)/shard_map/pallas_call | solution.py:392
  1.8 0.8 %collective-permute-start.2 = (f32[320,128]{1,0:T(8,128)S(1)}, f32[320,128]{1,0:T(8,128)S(1)}, u32[]{:S(2)}, u32[]{:S(2)}) collective-permute-start(f32[320,128]{1,0:T(8,128)S(1)} %get-tuple-element.20), channel_id=1, source_target_pairs={{0,1},{1,0},{2,3},{3,2},{4,5},{5,4},{6,7},{7,6},{8,9},{9,8},{10,11... | collective-permute-start | bytes 491528 | tf_op jit(solution)/shard_map/ppermute | solution.py:383
  2.5 1.3 %collective-permute-start.3 = (f32[320,128]{1,0:T(8,128)S(1)}, f32[320,128]{1,0:T(8,128)S(1)}, u32[]{:S(2)}, u32[]{:S(2)}) collective-permute-start(f32[320,128]{1,0:T(8,128)S(1)} %get-tuple-element.21), channel_id=1, source_target_pairs={{0,255},{1,2},{2,1},{3,4},{4,3},{5,6},{6,5},{7,8},{8,7},{9,10},{10... | collective-permute-start | bytes 491528 | tf_op jit(solution)/shard_map/ppermute | solution.py:383
  3.8 14.2 %all-to-all-start = ((f32[256,1,128]{2,1,0:T(1,128)}), f32[256,1,128]{2,1,0:T(1,128)S(1)}, u32[]{:S(2)}, u32[]{:S(2)}) async-start(f32[256,1,128]{2,1,0:T(1,128)} %bitcast.4), calls=%async_computation | async-start | bytes 262144 | tf_op jit(solution)/shard_map/all_to_all | solution.py:413
  18.0 2.7 %collective-permute-start = (f32[128,128]{1,0:T(8,128)S(1)}, f32[128,128]{1,0:T(8,128)S(1)}, u32[]{:S(2)}, u32[]{:S(2)}) collective-permute-start(f32[128,128]{1,0:T(8,128)S(1)} %get-tuple-element.18), channel_id=1, source_target_pairs={{0,16},{1,17},{2,18},{3,19},{4,20},{5,21},{6,22},{7,23},{8,24},{9,... | collective-permute-start | bytes 196616 | tf_op jit(solution)/shard_map/ppermute | solution.py:383
  20.7 5.1 %collective-permute-start.1 = (f32[128,128]{1,0:T(8,128)S(1)}, f32[128,128]{1,0:T(8,128)S(1)}, u32[]{:S(2)}, u32[]{:S(2)}) collective-permute-start(f32[128,128]{1,0:T(8,128)S(1)} %get-tuple-element.19), channel_id=1, source_target_pairs={{0,240},{1,241},{2,242},{3,243},{4,244},{5,245},{6,246},{7,247},{8... | collective-permute-start | bytes 196616 | tf_op jit(solution)/shard_map/ppermute | solution.py:383
  25.8 0.0 collective-permute-done.x_first_ref
  25.8 4.4 %collective-permute-done.1.x_second_ref = f32[128,128]{1,0:T(8,128)S(1)} collective-permute-done((f32[128,128]{1,0:T(8,128)S(1)}, f32[128,128]{1,0:T(8,128)S(1)}, u32[]{:S(2)}, u32[]{:S(2)}) %collective-permute-start.1) | collective-permute-done | bytes 65568 | tf_op jit(solution)/shard_map/ppermute | solution.py:383
  30.2 0.0 collective-permute-done.2.y_inner_ref.whole_inner_ref
  30.2 0.0 collective-permute-done.3.y_outer_ref.whole_outer_ref
  30.2 0.0 copy-start
  30.2 1.7 %shard_map.29 = (f32[512,128]{1,0:T(8,128)S(1)}, f32[192,128]{1,0:T(8,128)S(1)}, f32[192,128]{1,0:T(8,128)S(1)}) custom-call(f32[512,128]{1,0:T(8,128)S(1)} %get-tuple-element.17.cells_ref, f32[128,128]{1,0:T(8,128)S(1)} %collective-permute-done.x_first_ref, f32[128,128]{1,0:T(8,128)S(1)} %collective-permute-done.1.x_second_ref, ...), custom_call_target="tpu_custom_call" | custom-call | flops 20000000 | bytes 2500000 | tf_op jit(solution)/shard_map/pallas_call | solution.py:422
  31.9 0.9 %collective-permute-start.4 = (f32[192,128]{1,0:T(8,128)S(1)}, f32[192,128]{1,0:T(8,128)S(1)}, u32[]{:S(2)}, u32[]{:S(2)}) collective-permute-start(f32[192,128]{1,0:T(8,128)S(1)} %get-tuple-element.23), channel_id=1, source_target_pairs={{0,1},{1,0},{2,3},{3,2},{4,5},{5,4},{6,7},{7,6},{8,9},{9,8},{10,11... | collective-permute-start | bytes 294920 | tf_op jit(solution)/shard_map/ppermute | solution.py:383
  32.8 1.9 %collective-permute-start.5 = (f32[192,128]{1,0:T(8,128)S(1)}, f32[192,128]{1,0:T(8,128)S(1)}, u32[]{:S(2)}, u32[]{:S(2)}) collective-permute-start(f32[192,128]{1,0:T(8,128)S(1)} %get-tuple-element.24), channel_id=1, source_target_pairs={{1,2},{2,1},{3,4},{4,3},{5,6},{6,5},{7,8},{8,7},{9,10},{10,9},{11,... | collective-permute-start | bytes 294920 | tf_op jit(solution)/shard_map/ppermute | solution.py:383
  34.7 0.0 all-to-all-done
  34.7 0.0 collective-permute-done.4.inner_ref
  34.7 6.1 %collective-permute-done.5.outer_ref = f32[192,128]{1,0:T(8,128)S(1)} collective-permute-done((f32[192,128]{1,0:T(8,128)S(1)}, f32[192,128]{1,0:T(8,128)S(1)}, u32[]{:S(2)}, u32[]{:S(2)}) %collective-permute-start.5) | collective-permute-done | bytes 98336 | tf_op jit(solution)/shard_map/ppermute | solution.py:383
  40.8 0.0 copy-done
  40.8 1.0 %shard_map.30 = f32[8,24,512]{2,1,0:T(8,128)} custom-call(f32[256,128]{1,0:T(8,128)S(1)} %bitcast.10, f32[512,128]{1,0:T(8,128)S(1)} %get-tuple-element.16.whole_ref, f32[512,128]{1,0:T(8,128)S(1)} %get-tuple-element.22.change_ref, f32[320,128]{1,0:T(8,128)S(1)} %collective-permute-done.2.y_inner_ref.whole_inner_ref, ...), custom_call_target="tpu_custom_call" | custom-call | flops 1000000 | bytes 125000 | tf_op jit(solution)/shard_map/pallas_call | solution.py:431
Async XLA Ops:
  1.8 28.4 %collective-permute-start.2 = (f32[320,128]{1,0:T(8,128)S(1)}, f32[320,128]{1,0:T(8,128)S(1)}, u32[]{:S(2)}, u32[]{:S(2)}) collective-permute-start(f32[320,128]{1,0:T(8,128)S(1)} %get-tuple-element.20), channel_id=1, source_target_pairs={{0,1},{1,0},{2,3},{3,2},{4,5},{5,4},{6,7},{7,6},{8,9},{9,8},{10,11... | collective-permute-start | bytes 491528 | tf_op jit(solution)/shard_map/ppermute | solution.py:383
  2.5 27.7 %collective-permute-start.3 = (f32[320,128]{1,0:T(8,128)S(1)}, f32[320,128]{1,0:T(8,128)S(1)}, u32[]{:S(2)}, u32[]{:S(2)}) collective-permute-start(f32[320,128]{1,0:T(8,128)S(1)} %get-tuple-element.21), channel_id=1, source_target_pairs={{0,255},{1,2},{2,1},{3,4},{4,3},{5,6},{6,5},{7,8},{8,7},{9,10},{10... | collective-permute-start | bytes 491528 | tf_op jit(solution)/shard_map/ppermute | solution.py:383
  3.8 30.9 %all-to-all-start = ((f32[256,1,128]{2,1,0:T(1,128)}), f32[256,1,128]{2,1,0:T(1,128)S(1)}, u32[]{:S(2)}, u32[]{:S(2)}) async-start(f32[256,1,128]{2,1,0:T(1,128)} %bitcast.4), calls=%async_computation | async-start | bytes 262144 | tf_op jit(solution)/shard_map/all_to_all | solution.py:413
  18.0 7.8 %collective-permute-start = (f32[128,128]{1,0:T(8,128)S(1)}, f32[128,128]{1,0:T(8,128)S(1)}, u32[]{:S(2)}, u32[]{:S(2)}) collective-permute-start(f32[128,128]{1,0:T(8,128)S(1)} %get-tuple-element.18), channel_id=1, source_target_pairs={{0,16},{1,17},{2,18},{3,19},{4,20},{5,21},{6,22},{7,23},{8,24},{9,... | collective-permute-start | bytes 196616 | tf_op jit(solution)/shard_map/ppermute | solution.py:383
  20.7 9.5 %collective-permute-start.1 = (f32[128,128]{1,0:T(8,128)S(1)}, f32[128,128]{1,0:T(8,128)S(1)}, u32[]{:S(2)}, u32[]{:S(2)}) collective-permute-start(f32[128,128]{1,0:T(8,128)S(1)} %get-tuple-element.19), channel_id=1, source_target_pairs={{0,240},{1,241},{2,242},{3,243},{4,244},{5,245},{6,246},{7,247},{8... | collective-permute-start | bytes 196616 | tf_op jit(solution)/shard_map/ppermute | solution.py:383
  30.2 10.6 %copy-start = (s32[3072]{0:T(1024)S(1)}, s32[3072]{0:T(1024)}, u32[]{:S(2)}) copy-start(s32[3072]{0:T(1024)} %param.4) | copy-start | bytes 36868
  31.9 2.8 %collective-permute-start.4 = (f32[192,128]{1,0:T(8,128)S(1)}, f32[192,128]{1,0:T(8,128)S(1)}, u32[]{:S(2)}, u32[]{:S(2)}) collective-permute-start(f32[192,128]{1,0:T(8,128)S(1)} %get-tuple-element.23), channel_id=1, source_target_pairs={{0,1},{1,0},{2,3},{3,2},{4,5},{5,4},{6,7},{7,6},{8,9},{9,8},{10,11... | collective-permute-start | bytes 294920 | tf_op jit(solution)/shard_map/ppermute | solution.py:383
  32.8 8.0 %collective-permute-start.5 = (f32[192,128]{1,0:T(8,128)S(1)}, f32[192,128]{1,0:T(8,128)S(1)}, u32[]{:S(2)}, u32[]{:S(2)}) collective-permute-start(f32[192,128]{1,0:T(8,128)S(1)} %get-tuple-element.24), channel_id=1, source_target_pairs={{1,2},{2,1},{3,4},{4,3},{5,6},{6,5},{7,8},{8,7},{9,10},{10,9},{11,... | collective-permute-start | bytes 294920 | tf_op jit(solution)/shard_map/ppermute | solution.py:383
where the time goes:
time: 42 us; the launch traced here: 41.8 us
  starting transfers between devices  26.8 us (64%)
  waiting for transfers between devices  10.5 us (25%)
  Pallas kernels  4.48 us (11%)
    all_to_all x1, starting transfers between devices, per_device(): everyone = lax.all_to_all(fastest, AXES, 0, 0, tiled=True)  14.2 us
    ppermute x6, starting transfers between devices, swap(): return lax.ppermute(value, AXES, pairs)  12.6 us
    ppermute x6, waiting for transfers between devices, swap(): return lax.ppermute(value, AXES, pairs)  10.5 us
    pallas_call x1, Pallas kernels, per_device(): call(prepare_kernel, [HBM], [(SIDE, VMEM), (SIDE, VMEM), (SIDE + half, VM...  1.77 us
    pallas_call x1, Pallas kernels, per_device(): call(change_kernel, [VMEM] * 5, [(whole, VMEM), (half, VMEM), (half, VMEM...  1.71 us
    pallas_call x1, Pallas kernels, per_device(): call(place_kernel, [VMEM] * 8, [((FIELDS, CAP, TILES * LANES), HBM)], 10...  1.01 us
  transfers between devices with their start and end apart: 7, of which 2 were waited for; matrix products, arithmetic and copies ran while one was open for 0% of the time, Pallas kernels for 4%

commit v1 on v0

--- a/solution.py
+++ b/solution.py
@@ -22,6 +22,7 @@
 ROWS = 16
 HELD = 40
 SIDE = FIELDS * 2 * BE
+HALF = FIELDS * TILES * REACH
 PITCH = BE + 2
 APART = FIELDS + 1
 CHUNKS = 4
@@ -189,7 +190,6 @@
             for layer in range(2):
                 row = (2 * k + layer) * BE
                 ref[row : row + BE] = cells_ref[pl.ds(base + start + layer, BE, stride=BE)]
-    send_half(whole_ref, y_inner_ref, y_outer_ref, SIDE, odd)
     leaving.wait()
 
 
@@ -204,6 +204,7 @@
 
 def change_kernel(
     cells_ref,
+    whole_ref,
     x_first_ref,
     x_second_ref,
     y_inner_ref,
@@ -304,15 +305,14 @@
             base = (k * TILES + tile) * ROWS
             halves = turn(total[2 * tile][k], total[2 * tile + 1][k])
             own_ref[base : base + 8], own_ref[base + 8 : base + 16] = halves
-    send_half(own_ref, inner_ref, outer_ref, 0, odd)
+    send_half(whole_ref, inner_ref, outer_ref, 0, odd)
+    send_half(own_ref, inner_ref, outer_ref, HALF, odd)
 
 
 def place_kernel(
     fastest_ref,
     whole_ref,
     change_ref,
-    whole_inner_ref,
-    whole_outer_ref,
     inner_ref,
     outer_ref,
     owner_ref,
@@ -331,9 +331,9 @@
     live = lax.broadcasted_iota(jnp.int32, (CAP, LANES), 0) < count
     for row in range(FIELDS * TILES):
         there = slice(row * REACH, (row + 1) * REACH)
-        sent = slice(SIDE + row * REACH, SIDE + (row + 1) * REACH)
-        inner = whole_inner_ref[sent] - scale * inner_ref[there]
-        outer = whole_outer_ref[sent] - scale * outer_ref[there]
+        later = slice(HALF + row * REACH, HALF + (row + 1) * REACH)
+        inner = inner_ref[there] - scale * inner_ref[later]
+        outer = outer_ref[there] - scale * outer_ref[later]
         base = row * HELD
         held_ref[base + 8 : base + 8 + ROWS] = (
             whole_ref[rows_of(row)] - scale * change_ref[rows_of(row)]
@@ -387,7 +387,6 @@
     del new_slot
     devices = lax.axis_size(AXES)
     raw = prim.reshape(FIELDS, BLOCKS, TILES, LANES).transpose(1, 2, 0, 3).reshape(-1, LANES)
-    half = FIELDS * TILES * REACH
     whole = FIELDS * TILES * ROWS
     x_first, x_second, y_inner, y_outer, fastest, cells, conserved_own = call(
         prepare_kernel,
@@ -395,8 +394,8 @@
         [
             (SIDE, VMEM),
             (SIDE, VMEM),
-            (SIDE + half, VMEM),
-            (SIDE + half, VMEM),
+            (SIDE, VMEM),
+            (SIDE, VMEM),
             (devices, HBM),
             (FIELDS * BE * BE, VMEM),
             (whole, VMEM),
@@ -421,16 +420,16 @@
     y_inner = swap(y_inner, lambda i: i ^ 1, devices)
     own, to_inner, to_outer = call(
         change_kernel,
-        [VMEM] * 5,
-        [(whole, VMEM), (half, VMEM), (half, VMEM)],
+        [VMEM] * 6,
+        [(whole, VMEM), (2 * HALF, VMEM), (2 * HALF, VMEM)],
         2 * 10**7,
         [room(FIELDS * BE * PITCH)] * 3,
-    )(cells, x_first, x_second, y_inner, y_outer)
+    )(cells, conserved_own, x_first, x_second, y_inner, y_outer)
     from_outer = swap(to_outer, lambda i: within(i, i + 1 if i % 2 == 1 else i - 1), devices)
     from_inner = swap(to_inner, lambda i: i ^ 1, devices)
     (placed,) = call(
         place_kernel,
-        [VMEM] * 8,
+        [VMEM] * 6,
         [((FIELDS, CAP, TILES * LANES), HBM)],
         10**6,
         [
@@ -442,8 +441,6 @@
         everyone,
         conserved_own,
         own,
-        y_inner,
-        y_outer,
         from_inner,
         from_outer,
         new_owner.reshape(-1, LANES),

time: 42 us -> 36.6 us (0.87)
  the two profiles are of different devices: /device:TPU:57 before, /device:TPU:1 now
where the time goes in v1:
time: 36.6 us; the launch traced here: 36.4 us
  starting transfers between devices  25 us (68%)
  waiting for transfers between devices  6.88 us (19%)
  Pallas kernels  4.45 us (12%)
    ppermute x6, starting transfers between devices, swap(): return lax.ppermute(value, AXES, pairs)  16.9 us
    all_to_all x1, starting transfers between devices, per_device(): everyone = lax.all_to_all(fastest, AXES, 0, 0, tiled=True)  8.12 us
    all_to_all x1, waiting for transfers between devices, per_device(): everyone = lax.all_to_all(fastest, AXES, 0, 0, tiled=True)  6.86 us
    pallas_call x1, Pallas kernels, per_device(): call(prepare_kernel, [HBM], [(SIDE, VMEM), (SIDE, VMEM), (SIDE, VMEM), (S...  1.74 us
    pallas_call x1, Pallas kernels, per_device(): call(change_kernel, [VMEM] * 6, [(whole, VMEM), (2 * HALF, VMEM), (2 * HA...  1.71 us
    pallas_call x1, Pallas kernels, per_device(): call(place_kernel, [VMEM] * 6, [((FIELDS, CAP, TILES * LANES), HBM)], 10...  1.01 us
  transfers between devices with their start and end apart: 7, of which 1 were waited for; matrix products, arithmetic and copies ran while one was open for 0% of the time, Pallas kernels for 5%

profile of v1, /device:TPU:1, one launch (start us, length us, event | category | flops | bytes accessed | tf_op | source)
XLA Modules:
  0.0 36.4 jit_solution(15710879633160303340)
XLA Ops:
  0.0 1.7 %shard_map.28 = (f32[128,128]{1,0:T(8,128)S(1)}, f32[128,128]{1,0:T(8,128)S(1)}, f32[128,128]{1,0:T(8,128)S(1)}, f32[128,128]{1,0:T(8,128)S(1)}, f32[256,128]{1,...) custom-call(f32[384,128]{1,0:T(8,128)} %bitcast.12), custom_call_target="tpu_custom_call" | custom-call | flops 1000000 | bytes 125000 | tf_op jit(solution)/shard_map/pallas_call | solution.py:391
  1.7 3.9 %collective-permute-start = (f32[128,128]{1,0:T(8,128)S(1)}, f32[128,128]{1,0:T(8,128)S(1)}, u32[]{:S(2)}, u32[]{:S(2)}) collective-permute-start(f32[128,128]{1,0:T(8,128)S(1)} %get-tuple-element.18), channel_id=1, source_target_pairs={{0,16},{1,17},{2,18},{3,19},{4,20},{5,21},{6,22},{7,23},{8,24},{9,... | collective-permute-start | bytes 196616 | tf_op jit(solution)/shard_map/ppermute | solution.py:383
  5.6 6.4 %collective-permute-start.1 = (f32[128,128]{1,0:T(8,128)S(1)}, f32[128,128]{1,0:T(8,128)S(1)}, u32[]{:S(2)}, u32[]{:S(2)}) collective-permute-start(f32[128,128]{1,0:T(8,128)S(1)} %get-tuple-element.19), channel_id=1, source_target_pairs={{0,240},{1,241},{2,242},{3,243},{4,244},{5,245},{6,246},{7,247},{8... | collective-permute-start | bytes 196616 | tf_op jit(solution)/shard_map/ppermute | solution.py:383
  12.0 1.2 %collective-permute-start.2 = (f32[128,128]{1,0:T(8,128)S(1)}, f32[128,128]{1,0:T(8,128)S(1)}, u32[]{:S(2)}, u32[]{:S(2)}) collective-permute-start(f32[128,128]{1,0:T(8,128)S(1)} %get-tuple-element.20), channel_id=1, source_target_pairs={{0,1},{1,0},{2,3},{3,2},{4,5},{5,4},{6,7},{7,6},{8,9},{9,8},{10,11... | collective-permute-start | bytes 196616 | tf_op jit(solution)/shard_map/ppermute | solution.py:383
  13.3 1.2 %collective-permute-start.3 = (f32[128,128]{1,0:T(8,128)S(1)}, f32[128,128]{1,0:T(8,128)S(1)}, u32[]{:S(2)}, u32[]{:S(2)}) collective-permute-start(f32[128,128]{1,0:T(8,128)S(1)} %get-tuple-element.21), channel_id=1, source_target_pairs={{0,255},{1,2},{2,1},{3,4},{4,3},{5,6},{6,5},{7,8},{8,7},{9,10},{10... | collective-permute-start | bytes 196616 | tf_op jit(solution)/shard_map/ppermute | solution.py:383
  14.5 8.1 %all-to-all-start = ((f32[256,1,128]{2,1,0:T(1,128)}), f32[256,1,128]{2,1,0:T(1,128)S(1)}, u32[]{:S(2)}, u32[]{:S(2)}) async-start(f32[256,1,128]{2,1,0:T(1,128)} %bitcast.4), calls=%async_computation | async-start | bytes 262144 | tf_op jit(solution)/shard_map/all_to_all | solution.py:412
  22.6 0.0 collective-permute-done.x_first_ref
  22.6 0.0 collective-permute-done.1.x_second_ref
  22.6 0.0 collective-permute-done.2.y_inner_ref
  22.6 0.0 collective-permute-done.3.y_outer_ref
  22.6 0.0 copy-start
  22.6 1.7 %shard_map.29 = (f32[512,128]{1,0:T(8,128)S(1)}, f32[384,128]{1,0:T(8,128)S(1)}, f32[384,128]{1,0:T(8,128)S(1)}) custom-call(f32[512,128]{1,0:T(8,128)S(1)} %get-tuple-element.17.cells_ref, f32[512,128]{1,0:T(8,128)S(1)} %get-tuple-element.16.whole_ref, f32[128,128]{1,0:T(8,128)S(1)} %collective-permute-done.x_first_ref, ...), custom_call_target="tpu_custom_call" | custom-call | flops 20000000 | bytes 2500000 | tf_op jit(solution)/shard_map/pallas_call | solution.py:421
  24.4 2.2 %collective-permute-start.4 = (f32[384,128]{1,0:T(8,128)S(1)}, f32[384,128]{1,0:T(8,128)S(1)}, u32[]{:S(2)}, u32[]{:S(2)}) collective-permute-start(f32[384,128]{1,0:T(8,128)S(1)} %get-tuple-element.23), channel_id=1, source_target_pairs={{0,1},{1,0},{2,3},{3,2},{4,5},{5,4},{6,7},{7,6},{8,9},{9,8},{10,11... | collective-permute-start | bytes 589832 | tf_op jit(solution)/shard_map/ppermute | solution.py:383
  26.6 1.9 %collective-permute-start.5 = (f32[384,128]{1,0:T(8,128)S(1)}, f32[384,128]{1,0:T(8,128)S(1)}, u32[]{:S(2)}, u32[]{:S(2)}) collective-permute-start(f32[384,128]{1,0:T(8,128)S(1)} %get-tuple-element.24), channel_id=1, source_target_pairs={{1,2},{2,1},{3,4},{4,3},{5,6},{6,5},{7,8},{8,7},{9,10},{10,9},{11,... | collective-permute-start | bytes 589832 | tf_op jit(solution)/shard_map/ppermute | solution.py:383
  28.5 6.9 %all-to-all-done = f32[256,1,128]{2,1,0:T(1,128)S(1)} async-done(((f32[256,1,128]{2,1,0:T(1,128)}), f32[256,1,128]{2,1,0:T(1,128)S(1)}, u32[]{:S(2)}, u32[]{:S(2)}) %all-to-all-start) | async-done | bytes 131104 | tf_op jit(solution)/shard_map/all_to_all | solution.py:412
  35.4 0.0 collective-permute-done.4.inner_ref
  35.4 0.0 collective-permute-done.5.outer_ref
  35.4 0.0 copy-done
  35.4 1.0 %shard_map.30 = f32[8,24,512]{2,1,0:T(8,128)} custom-call(f32[256,128]{1,0:T(8,128)S(1)} %bitcast.10, f32[512,128]{1,0:T(8,128)S(1)} %get-tuple-element.16.whole_ref, f32[512,128]{1,0:T(8,128)S(1)} %get-tuple-element.22.change_ref, f32[384,128]{1,0:T(8,128)S(1)} %collective-permute-done.4.inner_ref, f32[384,128]{1,0:T(8,128)S(1)} %collective-permute-done.5.outer_ref, ...), custom_call_target="tpu_custom_call" | custom-call | flops 1000000 | bytes 125000 | tf_op jit(solution)/shard_map/pallas_call | solution.py:430
Async XLA Ops:
  1.7 20.8 %collective-permute-start = (f32[128,128]{1,0:T(8,128)S(1)}, f32[128,128]{1,0:T(8,128)S(1)}, u32[]{:S(2)}, u32[]{:S(2)}) collective-permute-start(f32[128,128]{1,0:T(8,128)S(1)} %get-tuple-element.18), channel_id=1, source_target_pairs={{0,16},{1,17},{2,18},{3,19},{4,20},{5,21},{6,22},{7,23},{8,24},{9,... | collective-permute-start | bytes 196616 | tf_op jit(solution)/shard_map/ppermute | solution.py:383
  5.6 17.0 %collective-permute-start.1 = (f32[128,128]{1,0:T(8,128)S(1)}, f32[128,128]{1,0:T(8,128)S(1)}, u32[]{:S(2)}, u32[]{:S(2)}) collective-permute-start(f32[128,128]{1,0:T(8,128)S(1)} %get-tuple-element.19), channel_id=1, source_target_pairs={{0,240},{1,241},{2,242},{3,243},{4,244},{5,245},{6,246},{7,247},{8... | collective-permute-start | bytes 196616 | tf_op jit(solution)/shard_map/ppermute | solution.py:383
  12.0 10.6 %collective-permute-start.2 = (f32[128,128]{1,0:T(8,128)S(1)}, f32[128,128]{1,0:T(8,128)S(1)}, u32[]{:S(2)}, u32[]{:S(2)}) collective-permute-start(f32[128,128]{1,0:T(8,128)S(1)} %get-tuple-element.20), channel_id=1, source_target_pairs={{0,1},{1,0},{2,3},{3,2},{4,5},{5,4},{6,7},{7,6},{8,9},{9,8},{10,11... | collective-permute-start | bytes 196616 | tf_op jit(solution)/shard_map/ppermute | solution.py:383
  13.3 9.3 %collective-permute-start.3 = (f32[128,128]{1,0:T(8,128)S(1)}, f32[128,128]{1,0:T(8,128)S(1)}, u32[]{:S(2)}, u32[]{:S(2)}) collective-permute-start(f32[128,128]{1,0:T(8,128)S(1)} %get-tuple-element.21), channel_id=1, source_target_pairs={{0,255},{1,2},{2,1},{3,4},{4,3},{5,6},{6,5},{7,8},{8,7},{9,10},{10... | collective-permute-start | bytes 196616 | tf_op jit(solution)/shard_map/ppermute | solution.py:383
  14.5 20.9 %all-to-all-start = ((f32[256,1,128]{2,1,0:T(1,128)}), f32[256,1,128]{2,1,0:T(1,128)S(1)}, u32[]{:S(2)}, u32[]{:S(2)}) async-start(f32[256,1,128]{2,1,0:T(1,128)} %bitcast.4), calls=%async_computation | async-start | bytes 262144 | tf_op jit(solution)/shard_map/all_to_all | solution.py:412
  22.6 12.8 %copy-start = (s32[3072]{0:T(1024)S(1)}, s32[3072]{0:T(1024)}, u32[]{:S(2)}) copy-start(s32[3072]{0:T(1024)} %param.4) | copy-start | bytes 36868
  24.4 11.0 %collective-permute-start.4 = (f32[384,128]{1,0:T(8,128)S(1)}, f32[384,128]{1,0:T(8,128)S(1)}, u32[]{:S(2)}, u32[]{:S(2)}) collective-permute-start(f32[384,128]{1,0:T(8,128)S(1)} %get-tuple-element.23), channel_id=1, source_target_pairs={{0,1},{1,0},{2,3},{3,2},{4,5},{5,4},{6,7},{7,6},{8,9},{9,8},{10,11... | collective-permute-start | bytes 589832 | tf_op jit(solution)/shard_map/ppermute | solution.py:383
  26.6 8.8 %collective-permute-start.5 = (f32[384,128]{1,0:T(8,128)S(1)}, f32[384,128]{1,0:T(8,128)S(1)}, u32[]{:S(2)}, u32[]{:S(2)}) collective-permute-start(f32[384,128]{1,0:T(8,128)S(1)} %get-tuple-element.24), channel_id=1, source_target_pairs={{1,2},{2,1},{3,4},{4,3},{5,6},{6,5},{7,8},{8,7},{9,10},{10,9},{11,... | collective-permute-start | bytes 589832 | tf_op jit(solution)/shard_map/ppermute | solution.py:383

commit v2 on v0

--- a/solution.py
+++ b/solution.py
@@ -158,20 +158,22 @@
     for tile in range(TILES):
         for half in range(2):
             state = [cell(k, tile, half) for k in range(FIELDS)]
-            field_sq = squared(state)
             speed = (
                 jnp.abs(state[1])
                 + jnp.abs(state[2])
                 + jnp.abs(state[3])
-                + 3.0 * sound(state[0], state[4], field_sq)
+                + 3.0 * sound(state[0], state[4], squared(state))
             )
             best = speed if best is None else jnp.maximum(best, speed)
-            for k, value in enumerate(conserved(state, field_sq)):
-                base = (k * TILES + tile) * ROWS + 8 * half
-                whole_ref[base : base + 8] = value
     filled_ref[...] = jnp.broadcast_to(jnp.max(best, keepdims=True), filled_ref.shape)
     leaving = pltpu.make_async_copy(filled_ref, fastest_ref, left)
     leaving.start()
+    for tile in range(TILES):
+        for half in range(2):
+            state = [cell(k, tile, half) for k in range(FIELDS)]
+            for k, value in enumerate(conserved(state, squared(state))):
+                base = (k * TILES + tile) * ROWS + 8 * half
+                whole_ref[base : base + 8] = value
     for k in range(FIELDS):
         for tile in range(TILES):
             halves = turn(cell(k, tile, 0), cell(k, tile, 1))
@@ -329,28 +331,26 @@
     first = jnp.clip(first, 0, BLOCKS) + 2
     scale = (0.5 * COURANT) / jnp.max(fastest_ref[...])
     live = lax.broadcasted_iota(jnp.int32, (CAP, LANES), 0) < count
-    for row in range(FIELDS * TILES):
-        there = slice(row * REACH, (row + 1) * REACH)
-        sent = slice(SIDE + row * REACH, SIDE + (row + 1) * REACH)
-        inner = whole_inner_ref[sent] - scale * inner_ref[there]
-        outer = whole_outer_ref[sent] - scale * outer_ref[there]
-        base = row * HELD
-        held_ref[base + 8 : base + 8 + ROWS] = (
-            whole_ref[rows_of(row)] - scale * change_ref[rows_of(row)]
+    copies = []
+    for k in range(FIELDS):
+        for row in range(k * TILES, (k + 1) * TILES):
+            there = slice(row * REACH, (row + 1) * REACH)
+            sent = slice(SIDE + row * REACH, SIDE + (row + 1) * REACH)
+            inner = whole_inner_ref[sent] - scale * inner_ref[there]
+            outer = whole_outer_ref[sent] - scale * outer_ref[there]
+            base = row * HELD
+            held_ref[base + 8 : base + 8 + ROWS] = (
+                whole_ref[rows_of(row)] - scale * change_ref[rows_of(row)]
+            )
+            held_ref[base + 2 : base + 8] = jnp.where(odd, inner, outer)
+            held_ref[base + 20 : base + 26] = jnp.where(odd, outer, inner)
+        for tile in range(TILES):
+            value = held_ref[pl.ds((k * TILES + tile) * HELD + first, CAP)]
+            ready_ref[k, :, tile * LANES : (tile + 1) * LANES] = jnp.where(live, value, 0.0)
+        copies.append(
+            pltpu.make_async_copy(ready_ref.at[pl.ds(k, 1)], out_ref.at[pl.ds(k, 1)], left.at[k])
         )
-        held_ref[base + 2 : base + 8] = jnp.where(odd, inner, outer)
-        held_ref[base + 20 : base + 26] = jnp.where(odd, outer, inner)
-    copies = []
-    for row in range(FIELDS * TILES):
-        k, tile = divmod(row, TILES)
-        value = held_ref[pl.ds(row * HELD + first, CAP)]
-        ready_ref[k, :, tile * LANES : (tile + 1) * LANES] = jnp.where(live, value, 0.0)
-        if (row + 1) % (2 * TILES) == 0:
-            two = pl.ds(k - 1, 2)
-            copies.append(
-                pltpu.make_async_copy(ready_ref.at[two], out_ref.at[two], left.at[k // 2])
-            )
-            copies[-1].start()
+        copies[-1].start()
     for copy in copies:
         copy.wait()
 
@@ -436,7 +436,7 @@
         [
             room(FIELDS * TILES * HELD),
             pltpu.VMEM((FIELDS, CAP, TILES * LANES), jnp.float32),
-            pltpu.SemaphoreType.DMA((FIELDS // 2,)),
+            pltpu.SemaphoreType.DMA((FIELDS,)),
         ],
     )(
         everyone,

time: 42 us -> 42 us (level)
  no operation moved by 1% of the time
where the time goes in v2:
time: 42 us; the launch traced here: 41.8 us
  starting transfers between devices  26.8 us (64%)
  waiting for transfers between devices  10.5 us (25%)
  Pallas kernels  4.5 us (11%)
    all_to_all x1, starting transfers between devices, per_device(): everyone = lax.all_to_all(fastest, AXES, 0, 0, tiled=True)  14.2 us
    ppermute x6, starting transfers between devices, swap(): return lax.ppermute(value, AXES, pairs)  12.6 us
    ppermute x6, waiting for transfers between devices, swap(): return lax.ppermute(value, AXES, pairs)  10.5 us
    pallas_call x1, Pallas kernels, per_device(): call(prepare_kernel, [HBM], [(SIDE, VMEM), (SIDE, VMEM), (SIDE + half, VM...  1.8 us
    pallas_call x1, Pallas kernels, per_device(): call(change_kernel, [VMEM] * 5, [(whole, VMEM), (half, VMEM), (half, VMEM...  1.71 us
    pallas_call x1, Pallas kernels, per_device(): call(place_kernel, [VMEM] * 8, [((FIELDS, CAP, TILES * LANES), HBM)], 10...  1 us
  transfers between devices with their start and end apart: 7, of which 2 were waited for; matrix products, arithmetic and copies ran while one was open for 0% of the time, Pallas kernels for 4%

profile of v2, /device:TPU:57, one launch (start us, length us, event | category | flops | bytes accessed | tf_op | source)
XLA Modules:
  0.0 41.8 jit_solution(846178838838589906)
XLA Ops:
  0.0 1.8 %shard_map.28 = (f32[128,128]{1,0:T(8,128)S(1)}, f32[128,128]{1,0:T(8,128)S(1)}, f32[320,128]{1,0:T(8,128)S(1)}, f32[320,128]{1,0:T(8,128)S(1)}, f32[256,128]{1,...) custom-call(f32[384,128]{1,0:T(8,128)} %bitcast.12), custom_call_target="tpu_custom_call" | custom-call | flops 1000000 | bytes 125000 | tf_op jit(solution)/shard_map/pallas_call | solution.py:392
  1.8 0.8 %collective-permute-start.2 = (f32[320,128]{1,0:T(8,128)S(1)}, f32[320,128]{1,0:T(8,128)S(1)}, u32[]{:S(2)}, u32[]{:S(2)}) collective-permute-start(f32[320,128]{1,0:T(8,128)S(1)} %get-tuple-element.20), channel_id=1, source_target_pairs={{0,1},{1,0},{2,3},{3,2},{4,5},{5,4},{6,7},{7,6},{8,9},{9,8},{10,11... | collective-permute-start | bytes 491528 | tf_op jit(solution)/shard_map/ppermute | solution.py:383
  2.6 1.3 %collective-permute-start.3 = (f32[320,128]{1,0:T(8,128)S(1)}, f32[320,128]{1,0:T(8,128)S(1)}, u32[]{:S(2)}, u32[]{:S(2)}) collective-permute-start(f32[320,128]{1,0:T(8,128)S(1)} %get-tuple-element.21), channel_id=1, source_target_pairs={{0,255},{1,2},{2,1},{3,4},{4,3},{5,6},{6,5},{7,8},{8,7},{9,10},{10... | collective-permute-start | bytes 491528 | tf_op jit(solution)/shard_map/ppermute | solution.py:383
  3.9 14.2 %all-to-all-start = ((f32[256,1,128]{2,1,0:T(1,128)}), f32[256,1,128]{2,1,0:T(1,128)S(1)}, u32[]{:S(2)}, u32[]{:S(2)}) async-start(f32[256,1,128]{2,1,0:T(1,128)} %bitcast.4), calls=%async_computation | async-start | bytes 262144 | tf_op jit(solution)/shard_map/all_to_all | solution.py:413
  18.0 2.7 %collective-permute-start = (f32[128,128]{1,0:T(8,128)S(1)}, f32[128,128]{1,0:T(8,128)S(1)}, u32[]{:S(2)}, u32[]{:S(2)}) collective-permute-start(f32[128,128]{1,0:T(8,128)S(1)} %get-tuple-element.18), channel_id=1, source_target_pairs={{0,16},{1,17},{2,18},{3,19},{4,20},{5,21},{6,22},{7,23},{8,24},{9,... | collective-permute-start | bytes 196616 | tf_op jit(solution)/shard_map/ppermute | solution.py:383
  20.8 5.1 %collective-permute-start.1 = (f32[128,128]{1,0:T(8,128)S(1)}, f32[128,128]{1,0:T(8,128)S(1)}, u32[]{:S(2)}, u32[]{:S(2)}) collective-permute-start(f32[128,128]{1,0:T(8,128)S(1)} %get-tuple-element.19), channel_id=1, source_target_pairs={{0,240},{1,241},{2,242},{3,243},{4,244},{5,245},{6,246},{7,247},{8... | collective-permute-start | bytes 196616 | tf_op jit(solution)/shard_map/ppermute | solution.py:383
  25.8 0.0 collective-permute-done.x_first_ref
  25.9 4.4 %collective-permute-done.1.x_second_ref = f32[128,128]{1,0:T(8,128)S(1)} collective-permute-done((f32[128,128]{1,0:T(8,128)S(1)}, f32[128,128]{1,0:T(8,128)S(1)}, u32[]{:S(2)}, u32[]{:S(2)}) %collective-permute-start.1) | collective-permute-done | bytes 65568 | tf_op jit(solution)/shard_map/ppermute | solution.py:383
  30.2 0.0 collective-permute-done.2.y_inner_ref.whole_inner_ref
  30.2 0.0 collective-permute-done.3.y_outer_ref.whole_outer_ref
  30.2 0.0 copy-start
  30.3 1.7 %shard_map.29 = (f32[512,128]{1,0:T(8,128)S(1)}, f32[192,128]{1,0:T(8,128)S(1)}, f32[192,128]{1,0:T(8,128)S(1)}) custom-call(f32[512,128]{1,0:T(8,128)S(1)} %get-tuple-element.17.cells_ref, f32[128,128]{1,0:T(8,128)S(1)} %collective-permute-done.x_first_ref, f32[128,128]{1,0:T(8,128)S(1)} %collective-permute-done.1.x_second_ref, ...), custom_call_target="tpu_custom_call" | custom-call | flops 20000000 | bytes 2500000 | tf_op jit(solution)/shard_map/pallas_call | solution.py:422
  32.0 0.9 %collective-permute-start.4 = (f32[192,128]{1,0:T(8,128)S(1)}, f32[192,128]{1,0:T(8,128)S(1)}, u32[]{:S(2)}, u32[]{:S(2)}) collective-permute-start(f32[192,128]{1,0:T(8,128)S(1)} %get-tuple-element.23), channel_id=1, source_target_pairs={{0,1},{1,0},{2,3},{3,2},{4,5},{5,4},{6,7},{7,6},{8,9},{9,8},{10,11... | collective-permute-start | bytes 294920 | tf_op jit(solution)/shard_map/ppermute | solution.py:383
  32.8 1.9 %collective-permute-start.5 = (f32[192,128]{1,0:T(8,128)S(1)}, f32[192,128]{1,0:T(8,128)S(1)}, u32[]{:S(2)}, u32[]{:S(2)}) collective-permute-start(f32[192,128]{1,0:T(8,128)S(1)} %get-tuple-element.24), channel_id=1, source_target_pairs={{1,2},{2,1},{3,4},{4,3},{5,6},{6,5},{7,8},{8,7},{9,10},{10,9},{11,... | collective-permute-start | bytes 294920 | tf_op jit(solution)/shard_map/ppermute | solution.py:383
  34.7 0.0 all-to-all-done
  34.7 0.0 collective-permute-done.4.inner_ref
  34.8 6.1 %collective-permute-done.5.outer_ref = f32[192,128]{1,0:T(8,128)S(1)} collective-permute-done((f32[192,128]{1,0:T(8,128)S(1)}, f32[192,128]{1,0:T(8,128)S(1)}, u32[]{:S(2)}, u32[]{:S(2)}) %collective-permute-start.5) | collective-permute-done | bytes 98336 | tf_op jit(solution)/shard_map/ppermute | solution.py:383
  40.8 0.0 copy-done
  40.9 1.0 %shard_map.30 = f32[8,24,512]{2,1,0:T(8,128)} custom-call(f32[256,128]{1,0:T(8,128)S(1)} %bitcast.10, f32[512,128]{1,0:T(8,128)S(1)} %get-tuple-element.16.whole_ref, f32[512,128]{1,0:T(8,128)S(1)} %get-tuple-element.22.change_ref, f32[320,128]{1,0:T(8,128)S(1)} %collective-permute-done.2.y_inner_ref.whole_inner_ref, ...), custom_call_target="tpu_custom_call" | custom-call | flops 1000000 | bytes 125000 | tf_op jit(solution)/shard_map/pallas_call | solution.py:431
Async XLA Ops:
  1.8 28.4 %collective-permute-start.2 = (f32[320,128]{1,0:T(8,128)S(1)}, f32[320,128]{1,0:T(8,128)S(1)}, u32[]{:S(2)}, u32[]{:S(2)}) collective-permute-start(f32[320,128]{1,0:T(8,128)S(1)} %get-tuple-element.20), channel_id=1, source_target_pairs={{0,1},{1,0},{2,3},{3,2},{4,5},{5,4},{6,7},{7,6},{8,9},{9,8},{10,11... | collective-permute-start | bytes 491528 | tf_op jit(solution)/shard_map/ppermute | solution.py:383
  2.6 27.7 %collective-permute-start.3 = (f32[320,128]{1,0:T(8,128)S(1)}, f32[320,128]{1,0:T(8,128)S(1)}, u32[]{:S(2)}, u32[]{:S(2)}) collective-permute-start(f32[320,128]{1,0:T(8,128)S(1)} %get-tuple-element.21), channel_id=1, source_target_pairs={{0,255},{1,2},{2,1},{3,4},{4,3},{5,6},{6,5},{7,8},{8,7},{9,10},{10... | collective-permute-start | bytes 491528 | tf_op jit(solution)/shard_map/ppermute | solution.py:383
  3.9 30.9 %all-to-all-start = ((f32[256,1,128]{2,1,0:T(1,128)}), f32[256,1,128]{2,1,0:T(1,128)S(1)}, u32[]{:S(2)}, u32[]{:S(2)}) async-start(f32[256,1,128]{2,1,0:T(1,128)} %bitcast.4), calls=%async_computation | async-start | bytes 262144 | tf_op jit(solution)/shard_map/all_to_all | solution.py:413
  18.0 7.8 %collective-permute-start = (f32[128,128]{1,0:T(8,128)S(1)}, f32[128,128]{1,0:T(8,128)S(1)}, u32[]{:S(2)}, u32[]{:S(2)}) collective-permute-start(f32[128,128]{1,0:T(8,128)S(1)} %get-tuple-element.18), channel_id=1, source_target_pairs={{0,16},{1,17},{2,18},{3,19},{4,20},{5,21},{6,22},{7,23},{8,24},{9,... | collective-permute-start | bytes 196616 | tf_op jit(solution)/shard_map/ppermute | solution.py:383
  20.8 9.5 %collective-permute-start.1 = (f32[128,128]{1,0:T(8,128)S(1)}, f32[128,128]{1,0:T(8,128)S(1)}, u32[]{:S(2)}, u32[]{:S(2)}) collective-permute-start(f32[128,128]{1,0:T(8,128)S(1)} %get-tuple-element.19), channel_id=1, source_target_pairs={{0,240},{1,241},{2,242},{3,243},{4,244},{5,245},{6,246},{7,247},{8... | collective-permute-start | bytes 196616 | tf_op jit(solution)/shard_map/ppermute | solution.py:383
  30.2 10.6 %copy-start = (s32[3072]{0:T(1024)S(1)}, s32[3072]{0:T(1024)}, u32[]{:S(2)}) copy-start(s32[3072]{0:T(1024)} %param.4) | copy-start | bytes 36868
  32.0 2.8 %collective-permute-start.4 = (f32[192,128]{1,0:T(8,128)S(1)}, f32[192,128]{1,0:T(8,128)S(1)}, u32[]{:S(2)}, u32[]{:S(2)}) collective-permute-start(f32[192,128]{1,0:T(8,128)S(1)} %get-tuple-element.23), channel_id=1, source_target_pairs={{0,1},{1,0},{2,3},{3,2},{4,5},{5,4},{6,7},{7,6},{8,9},{9,8},{10,11... | collective-permute-start | bytes 294920 | tf_op jit(solution)/shard_map/ppermute | solution.py:383
  32.8 8.0 %collective-permute-start.5 = (f32[192,128]{1,0:T(8,128)S(1)}, f32[192,128]{1,0:T(8,128)S(1)}, u32[]{:S(2)}, u32[]{:S(2)}) collective-permute-start(f32[192,128]{1,0:T(8,128)S(1)} %get-tuple-element.24), channel_id=1, source_target_pairs={{1,2},{2,1},{3,4},{4,3},{5,6},{6,5},{7,8},{8,7},{9,10},{10,9},{11,... | collective-permute-start | bytes 294920 | tf_op jit(solution)/shard_map/ppermute | solution.py:383
